TPU v7x, 256 devices: a whole 4x4x8 slice. The times are simulated.
256 devices in a mesh: section: 8 (over z), col: 32 (over y, x, core).
Axes of the slice: x: 4, y: 4, z: 8, core: 2. Of those that a mesh axis runs over, the one named last changes fastest.
Arguments:
- tiles: bfloat16 [1024, 12, 128, 128], P('col', None, 'section'), may hold values from 0.0099487305 to 1
- offsets: int32 [1024, 12], replicated, may hold values from -6 to 6, as said below
- counts: int32 [1024], replicated, may hold values from 1 to 12
- ranks: int32 [1024, 25, 128, 128], P('col', None, 'section'), may hold values from 0 to 3199, as said below
Outputs:
- pruned: bfloat16 [1024, 25, 128, 128], P('col', None, 'section')
Inputs may be any that keep to these rules, and one draw needn't show every extreme that they name: Within each panel the 12 offsets are distinct, each from -6 to 6. For every panel j and column c, ranks[j, :, c, :] holds each of 0 .. 3199 once.
All inputs are finite; a program needn't handle non-finite values.
Results may differ from a plain program's by a relative error of at most 0.001.
Values may be sent and summed in bfloat16 or wider, within the bound.
A program may use at most 128 MiB of HBM per device.

v0:
```python
import jax
import jax.numpy as jnp
from jax import lax
from jax.sharding import PartitionSpec as P

W = 6
TOPK = 256


def extended(shard, sides, width):
    for axis, dim in sides:
        count, length = (lax.axis_size(axis), shard.shape[dim])
        up = [(i, (i + 1) % count) for i in range(count - 1)]
        down = [(j, i) for i, j in up]
        last = lax.slice_in_dim(shard, length - width, length, axis=dim)
        initial = lax.slice_in_dim(shard, 0, width, axis=dim)
        before = lax.ppermute(last, axis, up)
        after = lax.ppermute(initial, axis, down)
        shard = jnp.concatenate([before, shard, after], axis=dim)
    return shard


def cut_along(shard, dim, count):
    before, after = (shard.shape[:dim], shard.shape[dim + 1 :])
    return jnp.moveaxis(shard.reshape(*before, count, -1, *after), dim, 0)


def piece_ends(length, count):
    unit = 8 if length >= 8 * count else 1
    return [length // unit * k // count * unit for k in range(1, count)]


def joined_along(tiles, dim):
    tiles = jnp.moveaxis(tiles, 0, dim)
    dims = tiles.shape
    return tiles.reshape(*dims[:dim], dims[dim] * dims[dim + 1], *dims[dim + 2 :])


def exchange_in_pieces(shard, axis, pieces, split_dim, concat_dim):
    tiles = cut_along(shard, split_dim, lax.axis_size(axis))
    split_at = max(range(1, max(2, tiles.ndim - 1)), key=lambda d: tiles.shape[d])
    outs = []
    for share in jnp.split(tiles, piece_ends(tiles.shape[split_at], pieces), axis=split_at):
        if share.size:
            outs.append(lax.all_to_all(share, axis, split_axis=0, concat_axis=0, tiled=True))
    return joined_along(jnp.concatenate(outs, axis=split_at), concat_dim)


def expand(own, own_off, own_cnt, center, global_panel, banded, band_off, band_cnt, total, bands):
    slots = own.shape[0]
    slot_ids = jnp.arange(slots, dtype=jnp.int32)
    where_at = center + W + own_off
    firsts = banded[where_at]
    first_off = band_off[where_at]
    first_cnt = band_cnt[where_at]
    row_own = global_panel + own_off
    ok_own = (slot_ids < own_cnt) & (row_own >= 0) & (row_own < total)
    row_first = row_own[:, None] + first_off
    ok_first = (slot_ids[None, :] < first_cnt[:, None]) & (row_first >= 0) & (row_first < total)
    weight = (ok_own[:, None] & ok_first).astype(jnp.float32)
    target = own_off[:, None] + first_off + 2 * W
    products = jnp.einsum("kcx,klxr->klcr", own, firsts, preferred_element_type=jnp.float32)
    weighted = products * weight[:, :, None, None]
    columns = own.shape[1]
    rows = own.shape[2]
    empty = jnp.zeros((bands, columns, rows), jnp.float32)
    return empty.at[target.reshape(-1)].add(weighted.reshape((slots * slots, columns, rows)))


def finish(expanded, rank_block):
    keep = rank_block < TOPK
    squared = jnp.where(keep, expanded * expanded, jnp.float32(0.0))
    totals = jnp.sum(squared, axis=(0, 2), keepdims=True)
    return (TOPK * squared / (totals + 1e-06)).astype(jnp.bfloat16)


def shards(tiles, offsets, counts, ranks):
    panels = tiles.shape[0]
    slots = tiles.shape[1]
    bands = ranks.shape[1]
    total = offsets.shape[0]
    first_panel = lax.axis_index("col") * panels
    pad_off = jnp.concatenate(
        [jnp.zeros((W, slots), jnp.int32), offsets, jnp.zeros((W, slots), jnp.int32)], axis=0
    )
    pad_cnt = jnp.concatenate(
        [jnp.zeros((W,), jnp.int32), counts, jnp.zeros((W,), jnp.int32)], axis=0
    )
    sections = lax.axis_size("section")
    share = panels // sections
    start = first_panel + lax.axis_index("section") * share
    sliced = extended(tiles, (("col", 0),), W)
    windows = jnp.stack([sliced[t * share : t * share + share + 2 * W] for t in range(sections)], 0)
    whole = lax.all_to_all(windows, "section", split_axis=0, concat_axis=3, tiled=True)[0]
    win_off = lax.dynamic_slice_in_dim(pad_off, start, share + 2 * W, 0)
    win_cnt = lax.dynamic_slice_in_dim(pad_cnt, start, share + 2 * W, 0)
    loc_off = lax.dynamic_slice_in_dim(offsets, start, share, 0)
    loc_cnt = lax.dynamic_slice_in_dim(counts, start, share, 0)

    def one_whole(packed):
        p_off, p_cnt, centre = packed
        own = lax.dynamic_index_in_dim(whole, centre + W, 0, False)
        return expand(
            own, p_off, p_cnt, centre, start + centre, whole, win_off, win_cnt, total, bands
        )

    expanded = lax.map(one_whole, (loc_off, loc_cnt, jnp.arange(share, dtype=jnp.int32)))
    back = exchange_in_pieces(expanded, "section", 2, 2, 0)

    def one_finish(packed):
        values, rank_block = packed
        return finish(values, rank_block)

    return lax.map(one_finish, (back, ranks))


def solution(mesh):
    placed = (P("col", None, "section", None), P(), P(), P("col", None, "section", None))
    return jax.shard_map(
        shards,
        mesh=mesh,
        in_specs=placed,
        out_specs=P("col", None, "section", None),
        check_vma=False,
    )
```

profile of v0, /device:TPU:14, one launch (start us, length us, event | category | flops | bytes accessed | tf_op | source)
XLA Modules:
  0.0 642.6 jit_solution(12305052271781320024)
XLA Ops:
  1.3 1.9 collective-permute-start
  3.2 3.6 collective-permute-start.1
  6.9 2.5 collective-permute-done
  19.7 8.6 %all-to-all-start = ((bf16[8,16,12,16,128]{4,3,2,1,0:T(8,128)(2,1)}), bf16[8,16,12,16,128]{4,3,2,1,0:T(8,128)(2,1)}, u32[]{:S(2)}, u32[]{:S(2)}) async-start(bf16[8,16,12,16,128]{4,3,2,1,0:T(8,128)(2,1)} %fusion.11), calls=%async_computation | async-start | bytes 12582912 | tf_op jit(solution)/shard_map/all_to_all | solution.py:94
  29.0 140.1 %all-to-all-done = bf16[8,16,12,16,128]{4,3,2,1,0:T(8,128)(2,1)} async-done(((bf16[8,16,12,16,128]{4,3,2,1,0:T(8,128)(2,1)}), bf16[8,16,12,16,128]{4,3,2,1,0:T(8,128)(2,1)}, u32[]{:S(2)}, u32[]{:S(2)}) %all-to-all-start) | async-done | bytes 6291488 | tf_op jit(solution)/shard_map/all_to_all | solution.py:94
  169.1 7.3 %copy.20 = bf16[1,16,12,8,16,128]{5,4,3,2,1,0:T(8,128)(2,1)} copy(bf16[1,16,12,8,16,128]{5,4,2,1,3,0:T(8,128)(2,1)} %bitcast.21) | data formatting | bytes 12582912 | tf_op jit(solution)/shard_map/all_to_all | solution.py:94
  176.4 199.5 %while.22 = (s32[]{:T(128)}, f32[4,25,128,128]{3,2,1,0:T(8,128)}, s32[4,12]{1,0:T(4,128)S(1)}, s32[4]{0:T(128)S(1)}, s32[16,12]{1,0:T(8,128)S(1)}, /*index=5*/bf...) while((s32[]{:T(128)}, f32[4,25,128,128]{3,2,1,0:T(8,128)}, ...), condition=%wide.region_2.3_spmd, body=%wide.region_0.2_spmd.sunk | while | flops 608701376 | bytes 76102056 | solution.py:107
  181.4 6.3 gather_fusion.2
  187.7 8.0 %broadcast_multiply_fusion.2 = f32[12,12,128,128]{3,2,1,0:T(8,128)} fusion(f32[12,12]{1,0:T(8,128)S(1)} %fusion.27, bf16[12,12,128,128]{3,2,1,0:T(8,128)(2,1)} %gather_fusion.2, bf16[16,12,128,128]{3,2,1,0:T(8,128)(2,1)} %get-tuple-element.310, s32[]{:T(128)S(6)} %select_n.67), kind=kOutput, calls=%fused_computation.10.clone.1 | convolution fusion | flops 606339072 | bytes 14549572 | tf_op jit(solution)/shard_map/while/body/eval_jaxpr/kcx,klxr->klcr/dot_general | solution.py:62
  195.8 9.6 %copy.29 = f32[144,128,128]{2,1,0:T(8,128)} copy(f32[144,128,128]{1,2,0:T(8,128)} %bitcast.73) | data formatting | bytes 18874368 | tf_op jit(solution)/shard_map/while/body/eval_jaxpr/reshape | solution.py:67
  205.8 19.1 %scatter_fusion = f32[25,128,128]{2,1,0:T(8,128)S(1)} fusion(f32[25,128,128]{2,1,0:T(8,128)S(1)} %broadcast.274, s32[144]{0:T(256)S(1)} %bitcast.79, f32[144,128,128]{2,1,0:T(8,128)} %copy.29), kind=kCustom, calls=%fused_computation.3.clone.1 | custom fusion | flops 2359296 | bytes 28312128 | tf_op jit(solution)/shard_map/while/body/eval_jaxpr/scatter-add | solution.py:67
  231.3 6.3 gather_fusion.2
  237.6 8.0 %broadcast_multiply_fusion.2 = f32[12,12,128,128]{3,2,1,0:T(8,128)} fusion(f32[12,12]{1,0:T(8,128)S(1)} %fusion.27, bf16[12,12,128,128]{3,2,1,0:T(8,128)(2,1)} %gather_fusion.2, bf16[16,12,128,128]{3,2,1,0:T(8,128)(2,1)} %get-tuple-element.310, s32[]{:T(128)S(6)} %select_n.67), kind=kOutput, calls=%fused_computation.10.clone.1 | convolution fusion | flops 606339072 | bytes 14549572 | tf_op jit(solution)/shard_map/while/body/eval_jaxpr/kcx,klxr->klcr/dot_general | solution.py:62
  245.6 9.6 %copy.29 = f32[144,128,128]{2,1,0:T(8,128)} copy(f32[144,128,128]{1,2,0:T(8,128)} %bitcast.73) | data formatting | bytes 18874368 | tf_op jit(solution)/shard_map/while/body/eval_jaxpr/reshape | solution.py:67
  255.6 19.1 %scatter_fusion = f32[25,128,128]{2,1,0:T(8,128)S(1)} fusion(f32[25,128,128]{2,1,0:T(8,128)S(1)} %broadcast.274, s32[144]{0:T(256)S(1)} %bitcast.79, f32[144,128,128]{2,1,0:T(8,128)} %copy.29), kind=kCustom, calls=%fused_computation.3.clone.1 | custom fusion | flops 2359296 | bytes 28312128 | tf_op jit(solution)/shard_map/while/body/eval_jaxpr/scatter-add | solution.py:67
  281.1 6.3 gather_fusion.2
  287.4 8.0 %broadcast_multiply_fusion.2 = f32[12,12,128,128]{3,2,1,0:T(8,128)} fusion(f32[12,12]{1,0:T(8,128)S(1)} %fusion.27, bf16[12,12,128,128]{3,2,1,0:T(8,128)(2,1)} %gather_fusion.2, bf16[16,12,128,128]{3,2,1,0:T(8,128)(2,1)} %get-tuple-element.310, s32[]{:T(128)S(6)} %select_n.67), kind=kOutput, calls=%fused_computation.10.clone.1 | convolution fusion | flops 606339072 | bytes 14549572 | tf_op jit(solution)/shard_map/while/body/eval_jaxpr/kcx,klxr->klcr/dot_general | solution.py:62
  295.5 9.6 %copy.29 = f32[144,128,128]{2,1,0:T(8,128)} copy(f32[144,128,128]{1,2,0:T(8,128)} %bitcast.73) | data formatting | bytes 18874368 | tf_op jit(solution)/shard_map/while/body/eval_jaxpr/reshape | solution.py:67
  305.5 19.1 %scatter_fusion = f32[25,128,128]{2,1,0:T(8,128)S(1)} fusion(f32[25,128,128]{2,1,0:T(8,128)S(1)} %broadcast.274, s32[144]{0:T(256)S(1)} %bitcast.79, f32[144,128,128]{2,1,0:T(8,128)} %copy.29), kind=kCustom, calls=%fused_computation.3.clone.1 | custom fusion | flops 2359296 | bytes 28312128 | tf_op jit(solution)/shard_map/while/body/eval_jaxpr/scatter-add | solution.py:67
  330.9 6.3 gather_fusion.2
  337.3 8.0 %broadcast_multiply_fusion.2 = f32[12,12,128,128]{3,2,1,0:T(8,128)} fusion(f32[12,12]{1,0:T(8,128)S(1)} %fusion.27, bf16[12,12,128,128]{3,2,1,0:T(8,128)(2,1)} %gather_fusion.2, bf16[16,12,128,128]{3,2,1,0:T(8,128)(2,1)} %get-tuple-element.310, s32[]{:T(128)S(6)} %select_n.67), kind=kOutput, calls=%fused_computation.10.clone.1 | convolution fusion | flops 606339072 | bytes 14549572 | tf_op jit(solution)/shard_map/while/body/eval_jaxpr/kcx,klxr->klcr/dot_general | solution.py:62
  345.3 9.6 %copy.29 = f32[144,128,128]{2,1,0:T(8,128)} copy(f32[144,128,128]{1,2,0:T(8,128)} %bitcast.73) | data formatting | bytes 18874368 | tf_op jit(solution)/shard_map/while/body/eval_jaxpr/reshape | solution.py:67
  355.3 19.1 %scatter_fusion = f32[25,128,128]{2,1,0:T(8,128)S(1)} fusion(f32[25,128,128]{2,1,0:T(8,128)S(1)} %broadcast.274, s32[144]{0:T(256)S(1)} %bitcast.79, f32[144,128,128]{2,1,0:T(8,128)} %copy.29), kind=kCustom, calls=%fused_computation.3.clone.1 | custom fusion | flops 2359296 | bytes 28312128 | tf_op jit(solution)/shard_map/while/body/eval_jaxpr/scatter-add | solution.py:67
  375.8 3.5 copy.27
  379.3 2.7 copy-done
  383.6 3.6 all-to-all-start.1
  387.2 4.8 split.9
  392.0 46.8 %all-to-all-done.1 = f32[8,4,8,16,128]{4,3,2,1,0:T(8,128)S(1)} async-done(((f32[8,4,8,16,128]{4,3,2,1,0:T(8,128)}), f32[8,4,8,16,128]{4,3,2,1,0:T(8,128)S(1)}, u32[]{:S(2)}, u32[]{:S(2)}) %all-to-all-start.1) | async-done | bytes 2097184 | tf_op jit(solution)/shard_map/all_to_all | solution.py:45
  438.8 4.6 all-to-all-start.2
  443.4 99.3 %all-to-all-done.2 = f32[8,4,17,16,128]{4,3,2,1,0:T(8,128)} async-done(((f32[8,4,17,16,128]{4,3,2,1,0:T(8,128)}), f32[8,4,17,16,128]{4,3,2,1,0:T(8,128)}, u32[]{:S(2)}, u32[]{:S(2)}) %all-to-all-start.2) | async-done | bytes 4456480 | tf_op jit(solution)/shard_map/all_to_all | solution.py:45
  542.7 5.6 pad_maximum_fusion
  548.3 94.4 %while.23 = (s32[]{:T(128)}, bf16[32,25,16,128]{3,2,1,0:T(8,128)(2,1)}, s32[32,25,16,128]{3,2,1,0:T(8,128)}, f32[32,25,16,128]{3,2,1,0:T(8,128)}, s32[]{:T(128)}) while((s32[]{:T(128)}, bf16[32,25,16,128]{3,2,1,0:T(8,128)(2,1)}, s32[32,25,16,128]{3,2,1,0:T(8,128)}, f32[32,25,16,128]{3,2,1,0:T(8,128)}, s32[]{:T(128)}) %tuple.56), condition=%wide.region_5.6_spmd, body=%wide.region_3.5_spmd.sunk | while | flops 512002 | bytes 922433 | solution.py:114
  (186 shorter events, 127.4 us)
Async XLA Ops:
  0.0 13.3 %copy-start.1 = (bf16[32,12,16,128]{3,2,1,0:T(8,128)(2,1)S(1)}, bf16[32,12,16,128]{3,2,1,0:T(8,128)(2,1)}, u32[]{:S(2)}) copy-start(bf16[32,12,16,128]{3,2,1,0:T(8,128)(2,1)} %param.8) | copy-start | bytes 4718596
  1.3 8.0 %collective-permute-start = (bf16[6,12,16,128]{3,2,1,0:T(8,128)(2,1)S(1)}, bf16[6,12,16,128]{3,2,1,0:T(8,128)(2,1)S(1)}, u32[]{:S(2)}, u32[]{:S(2)}) collective-permute-start(bf16[6,12,16,128]{3,2,1,0:T(8,128)(2,1)S(1)} %get-tuple-element.184), channel_id=1, source_target_pairs={{0,1},{1,2},{2,3},{3,4},{4,5},{5,6},{6,7},{7,8},{8,9},{9,10},{10,1... | collective-permute-start | bytes 884744 | tf_op jit(solution)/shard_map/ppermute | solution.py:17
  3.2 14.4 %collective-permute-start.1 = (bf16[6,12,16,128]{3,2,1,0:T(8,128)(2,1)S(1)}, bf16[6,12,16,128]{3,2,1,0:T(8,128)(2,1)S(1)}, u32[]{:S(2)}, u32[]{:S(2)}) collective-permute-start(bf16[6,12,16,128]{3,2,1,0:T(8,128)(2,1)S(1)} %get-tuple-element.183), channel_id=1, source_target_pairs={{1,0},{2,1},{3,2},{4,3},{5,4},{6,5},{7,6},{8,7},{9,8},{10,9},{11,1... | collective-permute-start | bytes 884744 | tf_op jit(solution)/shard_map/ppermute | solution.py:18
  19.7 8.6 %copy-start.2 = (s32[1024,12]{0,1:T(8,128)S(1)}, s32[1024,12]{0,1:T(8,128)}, u32[]{:S(2)}) copy-start(s32[1024,12]{0,1:T(8,128)} %param.9) | copy-start | bytes 147460
  19.7 8.9 %copy-start.3 = (s32[1024]{0:T(1024)S(1)}, s32[1024]{0:T(1024)}, u32[]{:S(2)}) copy-start(s32[1024]{0:T(1024)} %param.10) | copy-start | bytes 12292
  19.7 149.4 %all-to-all-start = ((bf16[8,16,12,16,128]{4,3,2,1,0:T(8,128)(2,1)}), bf16[8,16,12,16,128]{4,3,2,1,0:T(8,128)(2,1)}, u32[]{:S(2)}, u32[]{:S(2)}) async-start(bf16[8,16,12,16,128]{4,3,2,1,0:T(8,128)(2,1)} %fusion.11), calls=%async_computation | async-start | bytes 12582912 | tf_op jit(solution)/shard_map/all_to_all | solution.py:94
  379.3 2.7 copy-start
  383.6 55.2 %all-to-all-start.1 = ((f32[8,4,8,16,128]{4,3,2,1,0:T(8,128)}), f32[8,4,8,16,128]{4,3,2,1,0:T(8,128)S(1)}, u32[]{:S(2)}, u32[]{:S(2)}) async-start(f32[8,4,8,16,128]{4,3,2,1,0:T(8,128)} %split.8), calls=%async_computation.1 | async-start | bytes 4194304 | tf_op jit(solution)/shard_map/all_to_all | solution.py:45
  438.8 103.9 %all-to-all-start.2 = ((f32[8,4,17,16,128]{4,3,2,1,0:T(8,128)}), f32[8,4,17,16,128]{4,3,2,1,0:T(8,128)}, u32[]{:S(2)}, u32[]{:S(2)}) async-start(f32[8,4,17,16,128]{4,3,2,1,0:T(8,128)} %split.9), calls=%async_computation.2 | async-start | bytes 8912896 | tf_op jit(solution)/shard_map/all_to_all | solution.py:45
where the time goes:
time: 647 us; the launch traced here: 643 us
  waiting for transfers between devices  289 us (45%)
  other arithmetic  179 us (28%)
  local copies, waits for them, and re-layouts  112 us (17%)
  matrix products  32.2 us (5%)
  starting transfers between devices  22.4 us (3%)
  loops' own time  8.03 us (1%)
    all_to_all x2, waiting for transfers between devices, exchange_in_pieces(): lax.all_to_all(share, axis, split_axis=0, concat_axis=0, tiled=True)  146 us
    all_to_all x1, waiting for transfers between devices, shards(): lax.all_to_all(windows, 'section', split_axis=0, concat_axis=3, tiled=True)  140 us
    scatter-add x4, other arithmetic, expand(): empty.at[target.reshape(-1)]  76.5 us
    dynamic_update_slice x32, other arithmetic, shards(): return lax.map(one_finish, (back, ranks))  56.6 us
    reshape x4, local copies, waits for them, and re-layouts, expand(): weighted.reshape((slots * slots, columns, rows))  38.3 us
    reduce_sum x32, other arithmetic, finish(): totals = jnp.sum(squared, axis=(0, 2), keepdims=True)  37.5 us
    dot_general x4, matrix products, expand(): jnp.einsum('kcx,klxr->klcr', own, firsts, preferred_element_type=jnp.floa...  32.2 us
    gather x4, local copies, waits for them, and re-layouts, expand(): firsts = banded[where_at]  25.3 us
  transfers between devices with their start and end apart: 5, of which 4 were waited for; matrix products, arithmetic and copies ran while one was open for 2% of the time, Pallas kernels for 0%

commit v1 on v0

--- a/solution.py
+++ b/solution.py
@@ -5,6 +5,30 @@
 
 W = 6
 TOPK = 256
+
+
+def split_up(x, dim, size):
+    dims = x.shape
+    parts = x.reshape(*dims[:dim], size, dims[dim] // size, *dims[dim + 1 :])
+    return jnp.moveaxis(parts, dim, 0)
+
+
+def joined_along_2(pieces, dim):
+    lengths = list(pieces.shape[1:])
+    lengths[dim] *= pieces.shape[0]
+    return jnp.moveaxis(pieces, 0, dim).reshape(lengths)
+
+
+def exchange_directly(x, axis, split_dim, concat_dim):
+    size, index = (lax.axis_size(axis), lax.axis_index(axis))
+    tiles = split_up(x, split_dim, size)
+    whole = tiles
+    for step in range(1, size):
+        target, source = ((index + step) % size, (index - step) % size)
+        sent = lax.dynamic_index_in_dim(tiles, target, 0)
+        other = lax.ppermute(sent, axis, [(i, (i + step) % size) for i in range(size)])
+        whole = lax.dynamic_update_slice_in_dim(whole, other, source, axis=0)
+    return joined_along_2(whole, concat_dim)
 
 
 def extended(shard, sides, width):
@@ -91,7 +115,7 @@
     start = first_panel + lax.axis_index("section") * share
     sliced = extended(tiles, (("col", 0),), W)
     windows = jnp.stack([sliced[t * share : t * share + share + 2 * W] for t in range(sections)], 0)
-    whole = lax.all_to_all(windows, "section", split_axis=0, concat_axis=3, tiled=True)[0]
+    whole = exchange_directly(windows, "section", 0, 3)[0]
     win_off = lax.dynamic_slice_in_dim(pad_off, start, share + 2 * W, 0)
     win_cnt = lax.dynamic_slice_in_dim(pad_cnt, start, share + 2 * W, 0)
     loc_off = lax.dynamic_slice_in_dim(offsets, start, share, 0)

time: 647 us -> 654 us (1.011)
  waiting for transfers between devices: 289 us -> 252 us
  starting transfers between devices: 22.4 us -> 52.4 us
  local copies, waits for them, and re-layouts: 112 us -> 124 us
    all_to_all x1 -> x0, waiting for transfers between devices: 140 us -> none  [shards(): lax.all_to_all(windows, 'section', split_axis=0, concat_axis=3, tiled=True)]
    ppermute x0 -> x7, waiting for transfers between devices: none -> 99.5 us  [exchange_directly(): lax.ppermute(sent, axis, [(i, (i + step) % size) for i in range(size)])]
    ppermute x0 -> x7, starting transfers between devices: none -> 34.2 us  [exchange_directly(): lax.ppermute(sent, axis, [(i, (i + step) % size) for i in range(size)])]
    dynamic_update_slice x0 -> x7, local copies, waits for them, and re-layouts: none -> 14 us  [exchange_directly(): whole = lax.dynamic_update_slice_in_dim(whole, other, source, axis=0)]
    all_to_all x1 -> x0, starting transfers between devices: 8.6 us -> none  [shards(): lax.all_to_all(windows, 'section', split_axis=0, concat_axis=3, tiled=True)]
    all_to_all x1 -> x0, local copies, waits for them, and re-layouts: 7.25 us -> none  [shards(): lax.all_to_all(windows, 'section', split_axis=0, concat_axis=3, tiled=True)]
    transpose x0 -> x1, local copies, waits for them, and re-layouts: none -> 7.24 us  [joined_along_2(): return jnp.moveaxis(pieces, 0, dim).reshape(lengths)]
  transfers between devices with their start and end apart: 5 -> 11, of which waited for: 4 -> 9; matrix products, arithmetic and copies ran while one was open for 2% -> 3% of each run, Pallas kernels for 0% -> 0%
where the time goes in v1:
time: 654 us; the launch traced here: 649 us
  waiting for transfers between devices  252 us (39%)
  other arithmetic  180 us (28%)
  local copies, waits for them, and re-layouts  124 us (19%)
  starting transfers between devices  52.4 us (8%)
  matrix products  32.2 us (5%)
  loops' own time  8.16 us (1%)
    all_to_all x2, waiting for transfers between devices, exchange_in_pieces(): lax.all_to_all(share, axis, split_axis=0, concat_axis=0, tiled=True)  150 us
    ppermute x7, waiting for transfers between devices, exchange_directly(): lax.ppermute(sent, axis, [(i, (i + step) % size) for i in range(size)])  99.5 us
    scatter-add x4, other arithmetic, expand(): empty.at[target.reshape(-1)]  76.5 us
    dynamic_update_slice x32, other arithmetic, shards(): return lax.map(one_finish, (back, ranks))  56.6 us
    reshape x4, local copies, waits for them, and re-layouts, expand(): weighted.reshape((slots * slots, columns, rows))  38.3 us
    reduce_sum x32, other arithmetic, finish(): totals = jnp.sum(squared, axis=(0, 2), keepdims=True)  37.5 us
    ppermute x7, starting transfers between devices, exchange_directly(): lax.ppermute(sent, axis, [(i, (i + step) % size) for i in range(size)])  34.2 us
    dot_general x4, matrix products, expand(): jnp.einsum('kcx,klxr->klcr', own, firsts, preferred_element_type=jnp.floa...  32.2 us
  transfers between devices with their start and end apart: 11, of which 9 were waited for; matrix products, arithmetic and copies ran while one was open for 3% of the time, Pallas kernels for 0%

profile of v1, /device:TPU:14, one launch (start us, length us, event | category | flops | bytes accessed | tf_op | source)
XLA Modules:
  0.0 649.3 jit_solution(18236605334195354395)
XLA Ops:
  27.4 4.9 collective-permute-start.6
  32.5 7.9 %collective-permute-done.2 = bf16[1,1,16,12,16,128]{5,4,3,2,0,1:T(8,128)(2,1)} collective-permute-done((bf16[1,1,16,12,16,128]{5,4,3,2,0,1:T(8,128)(2,1)}, bf16[1,1,16,12,16,128]{5,4,3,2,0,1:T(8,128)(2,1)}, u32[]{:S(2)}, u32[]{:S(2)}) %collective-permute-start.2) | collective-permute-done | bytes 786464 | tf_op jit(solution)/shard_map/ppermute | solution.py:29
  43.7 17.0 %collective-permute-done.3 = bf16[1,1,16,12,16,128]{5,4,3,2,0,1:T(8,128)(2,1)} collective-permute-done((bf16[1,1,16,12,16,128]{5,4,3,2,0,1:T(8,128)(2,1)}, bf16[1,1,16,12,16,128]{5,4,3,2,0,1:T(8,128)(2,1)}, u32[]{:S(2)}, u32[]{:S(2)}) %collective-permute-start.3) | collective-permute-done | bytes 786464 | tf_op jit(solution)/shard_map/ppermute | solution.py:29
  60.7 16.8 %collective-permute-start.8 = (bf16[1,1,16,12,16,128]{5,4,3,2,0,1:T(8,128)(2,1)S(1)}, bf16[1,1,16,12,16,128]{5,4,3,2,0,1:T(8,128)(2,1)S(1)}, u32[]{:S(2)}, u32[]{:S(2)}) collective-permute-start(bf16[1,1,16,12,16,128]{5,4,3,2,0,1:T(8,128)(2,1)S(1)} %get-tuple-element.183), channel_id=1, source_target_pairs={{0,224},{32,0},{64,32},{96,64},{128,96},{160,128},{192,160},{224,1... | collective-permute-start | bytes 2359304 | tf_op jit(solution)/shard_map/ppermute | solution.py:29
  81.8 42.5 %collective-permute-done.4 = bf16[1,1,16,12,16,128]{5,4,3,2,0,1:T(8,128)(2,1)} collective-permute-done((bf16[1,1,16,12,16,128]{5,4,3,2,0,1:T(8,128)(2,1)}, bf16[1,1,16,12,16,128]{5,4,3,2,0,1:T(8,128)(2,1)}, u32[]{:S(2)}, u32[]{:S(2)}) %collective-permute-start.4) | collective-permute-done | bytes 786464 | tf_op jit(solution)/shard_map/ppermute | solution.py:29
  126.5 16.1 %collective-permute-done.5 = bf16[1,1,16,12,16,128]{5,4,3,2,0,1:T(8,128)(2,1)} collective-permute-done((bf16[1,1,16,12,16,128]{5,4,3,2,0,1:T(8,128)(2,1)S(1)}, bf16[1,1,16,12,16,128]{5,4,3,2,0,1:T(8,128)(2,1)}, u32[]{:S(2)}, u32[]{:S(2)}) %collective-permute-start.5) | collective-permute-done | bytes 786464 | tf_op jit(solution)/shard_map/ppermute | solution.py:29
  146.9 4.9 collective-permute-done.7
  154.0 11.1 %collective-permute-done.8 = bf16[1,1,16,12,16,128]{5,4,3,2,0,1:T(8,128)(2,1)S(1)} collective-permute-done((bf16[1,1,16,12,16,128]{5,4,3,2,0,1:T(8,128)(2,1)S(1)}, bf16[1,1,16,12,16,128]{5,4,3,2,0,1:T(8,128)(2,1)S(1)}, u32[]{:S(2)}, u32[]{:S(2)}) %collective-permute-start.8) | collective-permute-done | bytes 786464 | tf_op jit(solution)/shard_map/ppermute | solution.py:29
  166.1 7.2 %copy.20 = bf16[1,16,12,8,16,128]{5,4,3,2,1,0:T(8,128)(2,1)} copy(bf16[1,16,12,8,16,128]{5,4,2,1,3,0:T(8,128)(2,1)} %bitcast.91) | data formatting | bytes 12582912 | tf_op jit(solution)/shard_map/transpose | solution.py:19
  173.3 200.5 %while.22 = (s32[]{:T(128)}, f32[4,25,128,128]{3,2,1,0:T(8,128)}, s32[4,12]{1,0:T(4,128)S(1)}, s32[4]{0:T(128)S(1)}, s32[16,12]{1,0:T(8,128)S(1)}, /*index=5*/bf...) while((s32[]{:T(128)}, f32[4,25,128,128]{3,2,1,0:T(8,128)}, ...), condition=%wide.region_2.3_spmd, body=%wide.region_0.2_spmd.sunk | while | flops 608701376 | bytes 76102056 | solution.py:131
  178.6 6.3 gather_fusion.2
  184.9 8.0 %broadcast_multiply_fusion.2 = f32[12,12,128,128]{3,2,1,0:T(8,128)} fusion(f32[12,12]{1,0:T(8,128)S(1)} %fusion.27, bf16[12,12,128,128]{3,2,1,0:T(8,128)(2,1)} %gather_fusion.2, bf16[16,12,128,128]{3,2,1,0:T(8,128)(2,1)} %get-tuple-element.317, s32[]{:T(128)S(6)} %select_n.197), kind=kOutput, calls=%fused_computation.10.clone.1 | convolution fusion | flops 606339072 | bytes 14549572 | tf_op jit(solution)/shard_map/while/body/eval_jaxpr/kcx,klxr->klcr/dot_general | solution.py:86
  193.0 9.6 %copy.29 = f32[144,128,128]{2,1,0:T(8,128)} copy(f32[144,128,128]{1,2,0:T(8,128)} %bitcast.86) | data formatting | bytes 18874368 | tf_op jit(solution)/shard_map/while/body/eval_jaxpr/reshape | solution.py:91
  203.0 19.1 %scatter_fusion = f32[25,128,128]{2,1,0:T(8,128)S(1)} fusion(f32[25,128,128]{2,1,0:T(8,128)S(1)} %broadcast.288, s32[144]{0:T(256)S(1)} %bitcast.94, f32[144,128,128]{2,1,0:T(8,128)} %copy.29), kind=kCustom, calls=%fused_computation.3.clone.1 | custom fusion | flops 2359296 | bytes 28312128 | tf_op jit(solution)/shard_map/while/body/eval_jaxpr/scatter-add | solution.py:91
  228.7 6.3 gather_fusion.2
  235.0 8.0 %broadcast_multiply_fusion.2 = f32[12,12,128,128]{3,2,1,0:T(8,128)} fusion(f32[12,12]{1,0:T(8,128)S(1)} %fusion.27, bf16[12,12,128,128]{3,2,1,0:T(8,128)(2,1)} %gather_fusion.2, bf16[16,12,128,128]{3,2,1,0:T(8,128)(2,1)} %get-tuple-element.317, s32[]{:T(128)S(6)} %select_n.197), kind=kOutput, calls=%fused_computation.10.clone.1 | convolution fusion | flops 606339072 | bytes 14549572 | tf_op jit(solution)/shard_map/while/body/eval_jaxpr/kcx,klxr->klcr/dot_general | solution.py:86
  243.1 9.6 %copy.29 = f32[144,128,128]{2,1,0:T(8,128)} copy(f32[144,128,128]{1,2,0:T(8,128)} %bitcast.86) | data formatting | bytes 18874368 | tf_op jit(solution)/shard_map/while/body/eval_jaxpr/reshape | solution.py:91
  253.1 19.1 %scatter_fusion = f32[25,128,128]{2,1,0:T(8,128)S(1)} fusion(f32[25,128,128]{2,1,0:T(8,128)S(1)} %broadcast.288, s32[144]{0:T(256)S(1)} %bitcast.94, f32[144,128,128]{2,1,0:T(8,128)} %copy.29), kind=kCustom, calls=%fused_computation.3.clone.1 | custom fusion | flops 2359296 | bytes 28312128 | tf_op jit(solution)/shard_map/while/body/eval_jaxpr/scatter-add | solution.py:91
  278.8 6.3 gather_fusion.2
  285.1 8.0 %broadcast_multiply_fusion.2 = f32[12,12,128,128]{3,2,1,0:T(8,128)} fusion(f32[12,12]{1,0:T(8,128)S(1)} %fusion.27, bf16[12,12,128,128]{3,2,1,0:T(8,128)(2,1)} %gather_fusion.2, bf16[16,12,128,128]{3,2,1,0:T(8,128)(2,1)} %get-tuple-element.317, s32[]{:T(128)S(6)} %select_n.197), kind=kOutput, calls=%fused_computation.10.clone.1 | convolution fusion | flops 606339072 | bytes 14549572 | tf_op jit(solution)/shard_map/while/body/eval_jaxpr/kcx,klxr->klcr/dot_general | solution.py:86
  293.2 9.6 %copy.29 = f32[144,128,128]{2,1,0:T(8,128)} copy(f32[144,128,128]{1,2,0:T(8,128)} %bitcast.86) | data formatting | bytes 18874368 | tf_op jit(solution)/shard_map/while/body/eval_jaxpr/reshape | solution.py:91
  303.2 19.1 %scatter_fusion = f32[25,128,128]{2,1,0:T(8,128)S(1)} fusion(f32[25,128,128]{2,1,0:T(8,128)S(1)} %broadcast.288, s32[144]{0:T(256)S(1)} %bitcast.94, f32[144,128,128]{2,1,0:T(8,128)} %copy.29), kind=kCustom, calls=%fused_computation.3.clone.1 | custom fusion | flops 2359296 | bytes 28312128 | tf_op jit(solution)/shard_map/while/body/eval_jaxpr/scatter-add | solution.py:91
  328.9 6.3 gather_fusion.2
  335.2 8.0 %broadcast_multiply_fusion.2 = f32[12,12,128,128]{3,2,1,0:T(8,128)} fusion(f32[12,12]{1,0:T(8,128)S(1)} %fusion.27, bf16[12,12,128,128]{3,2,1,0:T(8,128)(2,1)} %gather_fusion.2, bf16[16,12,128,128]{3,2,1,0:T(8,128)(2,1)} %get-tuple-element.317, s32[]{:T(128)S(6)} %select_n.197), kind=kOutput, calls=%fused_computation.10.clone.1 | convolution fusion | flops 606339072 | bytes 14549572 | tf_op jit(solution)/shard_map/while/body/eval_jaxpr/kcx,klxr->klcr/dot_general | solution.py:86
  343.3 9.6 %copy.29 = f32[144,128,128]{2,1,0:T(8,128)} copy(f32[144,128,128]{1,2,0:T(8,128)} %bitcast.86) | data formatting | bytes 18874368 | tf_op jit(solution)/shard_map/while/body/eval_jaxpr/reshape | solution.py:91
  353.3 19.1 %scatter_fusion = f32[25,128,128]{2,1,0:T(8,128)S(1)} fusion(f32[25,128,128]{2,1,0:T(8,128)S(1)} %broadcast.288, s32[144]{0:T(256)S(1)} %bitcast.94, f32[144,128,128]{2,1,0:T(8,128)} %copy.29), kind=kCustom, calls=%fused_computation.3.clone.1 | custom fusion | flops 2359296 | bytes 28312128 | tf_op jit(solution)/shard_map/while/body/eval_jaxpr/scatter-add | solution.py:91
  381.6 8.1 %all-to-all-start = ((f32[8,4,8,16,128]{4,3,2,1,0:T(8,128)}), f32[8,4,8,16,128]{4,3,2,1,0:T(8,128)S(1)}, u32[]{:S(2)}, u32[]{:S(2)}) async-start(f32[8,4,8,16,128]{4,3,2,1,0:T(8,128)} %split.8), calls=%async_computation | async-start | bytes 4194304 | tf_op jit(solution)/shard_map/all_to_all | solution.py:69
  389.6 4.8 split.9
  394.4 47.9 %all-to-all-done = f32[8,4,8,16,128]{4,3,2,1,0:T(8,128)S(1)} async-done(((f32[8,4,8,16,128]{4,3,2,1,0:T(8,128)}), f32[8,4,8,16,128]{4,3,2,1,0:T(8,128)S(1)}, u32[]{:S(2)}, u32[]{:S(2)}) %all-to-all-start) | async-done | bytes 2097184 | tf_op jit(solution)/shard_map/all_to_all | solution.py:69
  446.9 102.4 %all-to-all-done.1 = f32[8,4,17,16,128]{4,3,2,1,0:T(8,128)} async-done(((f32[8,4,17,16,128]{4,3,2,1,0:T(8,128)}), f32[8,4,17,16,128]{4,3,2,1,0:T(8,128)}, u32[]{:S(2)}, u32[]{:S(2)}) %all-to-all-start.1) | async-done | bytes 4456480 | tf_op jit(solution)/shard_map/all_to_all | solution.py:69
  549.3 5.6 pad_maximum_fusion
  554.9 94.4 %while.23 = (s32[]{:T(128)}, bf16[32,25,16,128]{3,2,1,0:T(8,128)(2,1)}, s32[32,25,16,128]{3,2,1,0:T(8,128)}, f32[32,25,16,128]{3,2,1,0:T(8,128)}, s32[]{:T(128)}) while((s32[]{:T(128)}, bf16[32,25,16,128]{3,2,1,0:T(8,128)(2,1)}, s32[32,25,16,128]{3,2,1,0:T(8,128)}, f32[32,25,16,128]{3,2,1,0:T(8,128)}, s32[]{:T(128)}) %tuple.62), condition=%wide.region_5.6_spmd, body=%wide.region_3.5_spmd.sunk | while | flops 512002 | bytes 922433 | solution.py:138
  (208 shorter events, 171.2 us)
Async XLA Ops:
  0.0 11.6 %copy-start.2 = (bf16[32,12,16,128]{3,2,1,0:T(8,128)(2,1)S(1)}, bf16[32,12,16,128]{3,2,1,0:T(8,128)(2,1)}, u32[]{:S(2)}) copy-start(bf16[32,12,16,128]{3,2,1,0:T(8,128)(2,1)} %param.8) | copy-start | bytes 4718596
  1.3 8.0 %collective-permute-start = (bf16[6,12,16,128]{3,2,1,0:T(8,128)(2,1)S(1)}, bf16[6,12,16,128]{3,2,1,0:T(8,128)(2,1)S(1)}, u32[]{:S(2)}, u32[]{:S(2)}) collective-permute-start(bf16[6,12,16,128]{3,2,1,0:T(8,128)(2,1)S(1)} %get-tuple-element.191), channel_id=1, source_target_pairs={{0,1},{1,2},{2,3},{3,4},{4,5},{5,6},{6,7},{7,8},{8,9},{9,10},{10,1... | collective-permute-start | bytes 884744 | tf_op jit(solution)/shard_map/ppermute | solution.py:41
  3.2 9.2 %collective-permute-start.1 = (bf16[6,12,16,128]{3,2,1,0:T(8,128)(2,1)S(1)}, bf16[6,12,16,128]{3,2,1,0:T(8,128)(2,1)S(1)}, u32[]{:S(2)}, u32[]{:S(2)}) collective-permute-start(bf16[6,12,16,128]{3,2,1,0:T(8,128)(2,1)S(1)} %get-tuple-element.190), channel_id=1, source_target_pairs={{1,0},{2,1},{3,2},{4,3},{5,4},{6,5},{7,6},{8,7},{9,8},{10,9},{11,1... | collective-permute-start | bytes 884744 | tf_op jit(solution)/shard_map/ppermute | solution.py:42
  12.6 19.7 %copy-start.3 = (s32[1024,12]{0,1:T(8,128)S(1)}, s32[1024,12]{0,1:T(8,128)}, u32[]{:S(2)}) copy-start(s32[1024,12]{0,1:T(8,128)} %param.9) | copy-start | bytes 147460
  12.7 30.6 %copy-start.4 = (s32[1024]{0:T(1024)S(1)}, s32[1024]{0:T(1024)}, u32[]{:S(2)}) copy-start(s32[1024]{0:T(1024)} %param.10) | copy-start | bytes 12292
  12.9 2.7 copy-start.1
  17.6 22.7 %collective-permute-start.2 = (bf16[1,1,16,12,16,128]{5,4,3,2,0,1:T(8,128)(2,1)}, bf16[1,1,16,12,16,128]{5,4,3,2,0,1:T(8,128)(2,1)}, u32[]{:S(2)}, u32[]{:S(2)}) collective-permute-start(bf16[1,1,16,12,16,128]{5,4,3,2,0,1:T(8,128)(2,1)} %get-tuple-element.189), channel_id=1, source_target_pairs={{0,32},{32,64},{64,96},{96,128},{128,160},{160,192},{192,224},{224... | collective-permute-start | bytes 2359304 | tf_op jit(solution)/shard_map/ppermute | solution.py:29
  19.6 41.1 %collective-permute-start.3 = (bf16[1,1,16,12,16,128]{5,4,3,2,0,1:T(8,128)(2,1)}, bf16[1,1,16,12,16,128]{5,4,3,2,0,1:T(8,128)(2,1)}, u32[]{:S(2)}, u32[]{:S(2)}) collective-permute-start(bf16[1,1,16,12,16,128]{5,4,3,2,0,1:T(8,128)(2,1)} %get-tuple-element.188), channel_id=1, source_target_pairs={{0,64},{32,96},{64,128},{96,160},{128,192},{160,224},{192,0},{224,... | collective-permute-start | bytes 2359304 | tf_op jit(solution)/shard_map/ppermute | solution.py:29
  22.8 101.5 %collective-permute-start.4 = (bf16[1,1,16,12,16,128]{5,4,3,2,0,1:T(8,128)(2,1)}, bf16[1,1,16,12,16,128]{5,4,3,2,0,1:T(8,128)(2,1)}, u32[]{:S(2)}, u32[]{:S(2)}) collective-permute-start(bf16[1,1,16,12,16,128]{5,4,3,2,0,1:T(8,128)(2,1)} %get-tuple-element.187), channel_id=1, source_target_pairs={{0,96},{32,128},{64,160},{96,192},{128,224},{160,0},{192,32},{224,... | collective-permute-start | bytes 2359304 | tf_op jit(solution)/shard_map/ppermute | solution.py:29
  26.9 115.7 %collective-permute-start.5 = (bf16[1,1,16,12,16,128]{5,4,3,2,0,1:T(8,128)(2,1)S(1)}, bf16[1,1,16,12,16,128]{5,4,3,2,0,1:T(8,128)(2,1)}, u32[]{:S(2)}, u32[]{:S(2)}) collective-permute-start(bf16[1,1,16,12,16,128]{5,4,3,2,0,1:T(8,128)(2,1)S(1)} %get-tuple-element.186), channel_id=1, source_target_pairs={{0,128},{32,160},{64,192},{96,224},{128,0},{160,32},{192,64},{224,... | collective-permute-start | bytes 2359304 | tf_op jit(solution)/shard_map/ppermute | solution.py:29
  27.4 117.4 %collective-permute-start.6 = (bf16[1,1,16,12,16,128]{5,4,3,2,0,1:T(8,128)(2,1)S(1)}, bf16[1,1,16,12,16,128]{5,4,3,2,0,1:T(8,128)(2,1)}, u32[]{:S(2)}, u32[]{:S(2)}) collective-permute-start(bf16[1,1,16,12,16,128]{5,4,3,2,0,1:T(8,128)(2,1)S(1)} %get-tuple-element.185), channel_id=1, source_target_pairs={{0,160},{32,192},{64,224},{96,0},{128,32},{160,64},{192,96},{224,1... | collective-permute-start | bytes 2359304 | tf_op jit(solution)/shard_map/ppermute | solution.py:29
  40.4 111.4 %collective-permute-start.7 = (bf16[1,1,16,12,16,128]{5,4,3,2,0,1:T(8,128)(2,1)S(1)}, bf16[1,1,16,12,16,128]{5,4,3,2,0,1:T(8,128)(2,1)}, u32[]{:S(2)}, u32[]{:S(2)}) collective-permute-start(bf16[1,1,16,12,16,128]{5,4,3,2,0,1:T(8,128)(2,1)S(1)} %get-tuple-element.184), channel_id=1, source_target_pairs={{0,192},{32,224},{64,0},{96,32},{128,64},{160,96},{192,128},{224,1... | collective-permute-start | bytes 2359304 | tf_op jit(solution)/shard_map/ppermute | solution.py:29
  60.7 104.4 %collective-permute-start.8 = (bf16[1,1,16,12,16,128]{5,4,3,2,0,1:T(8,128)(2,1)S(1)}, bf16[1,1,16,12,16,128]{5,4,3,2,0,1:T(8,128)(2,1)S(1)}, u32[]{:S(2)}, u32[]{:S(2)}) collective-permute-start(bf16[1,1,16,12,16,128]{5,4,3,2,0,1:T(8,128)(2,1)S(1)} %get-tuple-element.183), channel_id=1, source_target_pairs={{0,224},{32,0},{64,32},{96,64},{128,96},{160,128},{192,160},{224,1... | collective-permute-start | bytes 2359304 | tf_op jit(solution)/shard_map/ppermute | solution.py:29
  377.3 2.7 copy-start
  381.6 60.7 %all-to-all-start = ((f32[8,4,8,16,128]{4,3,2,1,0:T(8,128)}), f32[8,4,8,16,128]{4,3,2,1,0:T(8,128)S(1)}, u32[]{:S(2)}, u32[]{:S(2)}) async-start(f32[8,4,8,16,128]{4,3,2,1,0:T(8,128)} %split.8), calls=%async_computation | async-start | bytes 4194304 | tf_op jit(solution)/shard_map/all_to_all | solution.py:69
  442.3 107.0 %all-to-all-start.1 = ((f32[8,4,17,16,128]{4,3,2,1,0:T(8,128)}), f32[8,4,17,16,128]{4,3,2,1,0:T(8,128)}, u32[]{:S(2)}, u32[]{:S(2)}) async-start(f32[8,4,17,16,128]{4,3,2,1,0:T(8,128)} %split.9), calls=%async_computation.1 | async-start | bytes 8912896 | tf_op jit(solution)/shard_map/all_to_all | solution.py:69
